TPU v7x, 32 devices: a whole 2x2x4 slice. The times are simulated.
32 devices in a mesh: lon: 16 (over z, y, x), lat: 2 (over core).
Axes of the slice: x: 2, y: 2, z: 4, core: 2. Of those that a mesh axis runs over, the one named last changes fastest.
Arguments:
- u_vel: float32 [40, 128, 1024], P(None, 'lon', 'lat'), may hold values from -6 to 6
- v_vel: float32 [40, 128, 1024], P(None, 'lon', 'lat'), may hold values from -6 to 6
- thickness: float32 [40], replicated, may hold values from 0.5 to 2
- depth: float32 [128, 1024], P('lon', 'lat'), may hold values from 0.5 to 2
- sea_mask: int32 [128, 1024], P('lon', 'lat'), may hold values 0 or 1
- damping: float32 [128, 1024], P('lon', 'lat'), may hold values from 0.1 to 2
- eta_prev: float32 [128, 1024], P('lon', 'lat'), may hold values from -6 to 6
Outputs:
- surface: float32 [128, 1024], P('lon', 'lat')
- residual: float32 [128, 1024], P('lon', 'lat')
All inputs are finite; a program needn't handle non-finite values. No bound on the sum of `sea_mask` on one device may be relied on, other than what follows from the above.
Results may differ from a plain program's by a relative error of at most 0.0003.
Values sent between devices are 32-bit elements; how exact they have to be, the bound alone decides.
A program may use at most 64 MiB of HBM per device.

v0:
```python
import math
import jax
import jax.numpy as jnp
from jax import lax
from jax.sharding import PartitionSpec as P

LEVELS = 40
ITERS = 3


def extended_2(block, sides, width):
    for axis, dim in sides:
        count = lax.axis_size(axis)
        forward = [(i, i + 1) for i in range(count - 1)]
        forward.append((count - 1, 0))
        backward = [(target, source) for source, target in forward]
        low = lax.ppermute(
            lax.slice_in_dim(block, block.shape[dim] - width, None, axis=dim), axis, forward
        )
        high = lax.ppermute(lax.slice_in_dim(block, 0, width, axis=dim), axis, backward)
        block = jnp.concatenate([low, block, high], axis=dim)
    return block


def close_walls(extended, width):
    position = lax.axis_index("lat")
    count = lax.axis_size("lat")
    total = extended.shape[-1]
    column = lax.broadcasted_iota(jnp.int32, extended.shape, extended.ndim - 1)
    bottom = jnp.logical_and(position == 0, column < width)
    top = jnp.logical_and(position == count - 1, column >= total - width)
    keep = jnp.logical_not(jnp.logical_or(bottom, top)).astype(jnp.float32)
    return extended * keep


def column_sum(thickness, velocity):
    return jnp.einsum("k,kxy->xy", thickness, velocity, precision=lax.Precision.HIGHEST) * (
        1.0 / math.sqrt(LEVELS)
    )


def apply_padded(padded, diag, coef_east, coef_west, coef_north, coef_south):
    field = padded[1:-1, 1:-1]
    result = diag * field - coef_east * padded[2:, 1:-1] - coef_west * padded[:-2, 1:-1]
    return result - coef_north * padded[1:-1, 2:] - coef_south * padded[1:-1, :-2]


def operate(field, diag, coef_east, coef_west, coef_north, coef_south):
    padded = extended_2(field, (("lon", 0), ("lat", 1)), 1)
    return apply_padded(padded, diag, coef_east, coef_west, coef_north, coef_south)


def body(u_vel, v_vel, thickness, depth, sea_mask, damping, eta_prev):
    wet = sea_mask.astype(jnp.float32)
    width = 2
    surface_fields = [depth, wet, damping, eta_prev]
    stacked = jnp.stack(
        [column_sum(thickness, u_vel), column_sum(thickness, v_vel)] + surface_fields, axis=0
    )
    extended = extended_2(stacked, (("lon", 1), ("lat", 2)), width)
    extended = close_walls(extended, width)
    sum_east = extended[0]
    sum_north = extended[1]
    rest = extended[2:]
    depth_ext = rest[0]
    wet_ext = rest[1]
    wet_x = wet_ext[:-1, :] * wet_ext[1:, :]
    face_x = wet_x * 0.5 * (depth_ext[:-1, :] + depth_ext[1:, :])
    flux_x = wet_x * sum_east[:-1, :]
    wet_y = wet_ext[:, :-1] * wet_ext[:, 1:]
    face_y = wet_y * 0.5 * (depth_ext[:, :-1] + depth_ext[:, 1:])
    flux_y = wet_y * sum_north[:, :-1]
    coef_east, coef_west = (face_x[1:, 1:-1], face_x[:-1, 1:-1])
    coef_north, coef_south = (face_y[1:-1, 1:], face_y[1:-1, :-1])
    diverge = flux_x[1:, 1:-1] - flux_x[:-1, 1:-1] + flux_y[1:-1, 1:] - flux_y[1:-1, :-1]
    wet_mid = wet_ext[1:-1, 1:-1]
    damp_mid = rest[2][1:-1, 1:-1]
    rhs_mid = wet_mid * (damp_mid * rest[3][1:-1, 1:-1] - diverge)
    diag_mid = damp_mid + coef_east + coef_west + coef_north + coef_south
    precond_mid = rhs_mid / jnp.where(diag_mid > 0.0, diag_mid, 1.0)
    coef_east, coef_west = (coef_east[1:-1, 1:-1], coef_west[1:-1, 1:-1])
    coef_north, coef_south = (coef_north[1:-1, 1:-1], coef_south[1:-1, 1:-1])
    rhs = rhs_mid[1:-1, 1:-1]
    diag = diag_mid[1:-1, 1:-1]

    def sums(residual, precond, image):
        return lax.psum((jnp.sum(residual * precond), jnp.sum(image * precond)), ("lon", "lat"))

    surface = jnp.zeros_like(rhs)
    residual = rhs
    precond = precond_mid[1:-1, 1:-1]
    image = apply_padded(precond_mid, diag, coef_east, coef_west, coef_north, coef_south)
    gamma_now, delta_now = sums(residual, precond, image)
    step_size = gamma_now / delta_now
    direction, along_dir = (precond, image)
    for sweep in range(ITERS):
        surface = surface + step_size * direction
        residual = residual - step_size * along_dir
        if sweep + 1 < ITERS:
            precond = residual / diag
            image = operate(precond, diag, coef_east, coef_west, coef_north, coef_south)
            gamma_next, delta_now = sums(residual, precond, image)
            ratio_next = gamma_next / gamma_now
            step_size = gamma_next / (delta_now - ratio_next * gamma_next / step_size)
            direction = precond + ratio_next * direction
            along_dir = image + ratio_next * along_dir
            gamma_now = gamma_next
    return (surface, residual)


def solution(mesh):
    placed = (
        P(None, "lon", "lat"),
        P(None, "lon", "lat"),
        P(),
        P("lon", "lat"),
        P("lon", "lat"),
        P("lon", "lat"),
        P("lon", "lat"),
    )
    return jax.shard_map(
        body,
        mesh=mesh,
        in_specs=placed,
        out_specs=(P("lon", "lat"), P("lon", "lat")),
        check_vma=False,
    )
```

profile of v0, /device:TPU:0, one launch (start us, length us, event | category | flops | bytes accessed | tf_op | source)
XLA Modules:
  0.0 168.9 jit_solution(18303557818421487441)
XLA Ops:
  0.6 0.0 copy-start
  0.7 1.1 copy-done
  1.7 1.4 fusion.2
  3.2 0.8 fusion
  4.0 0.0 copy-start.2
  4.0 0.7 copy-done.2
  4.7 0.7 copy-done.3
  5.4 0.7 copy-done.4
  6.1 0.7 copy-done.5
  6.9 3.0 %collective-permute-start = (f32[6,2,512]{2,1,0:T(2,128)S(1)}, f32[6,2,512]{2,1,0:T(2,128)S(1)}, u32[]{:S(2)}, u32[]{:S(2)}) collective-permute-start(f32[6,2,512]{2,1,0:T(2,128)S(1)} %get-tuple-element.33), channel_id=1, source_target_pairs={{0,2},{2,4},{4,6},{6,8},{8,10},{10,12},{12,14},{14,16},{16,18},{18... | collective-permute-start | bytes 73736 | tf_op jit(solution)/shard_map/ppermute | solution.py:17
  9.9 4.1 %collective-permute-start.1 = (f32[6,2,512]{2,1,0:T(2,128)S(1)}, f32[6,2,512]{2,1,0:T(2,128)S(1)}, u32[]{:S(2)}, u32[]{:S(2)}) collective-permute-start(f32[6,2,512]{2,1,0:T(2,128)S(1)} %get-tuple-element.34), channel_id=1, source_target_pairs={{2,0},{4,2},{6,4},{8,6},{10,8},{12,10},{14,12},{16,14},{18,16},{20... | collective-permute-start | bytes 73736 | tf_op jit(solution)/shard_map/ppermute | solution.py:20
  14.0 1.7 %collective-permute-done = f32[6,2,512]{2,1,0:T(2,128)S(1)} collective-permute-done((f32[6,2,512]{2,1,0:T(2,128)S(1)}, f32[6,2,512]{2,1,0:T(2,128)S(1)}, u32[]{:S(2)}, u32[]{:S(2)}) %collective-permute-start) | collective-permute-done | bytes 24608 | tf_op jit(solution)/shard_map/ppermute | solution.py:17
  15.7 0.0 collective-permute-done.1
  15.7 0.1 pad_maximum_fusion.2
  15.8 0.1 collective-permute-start.2
  15.9 0.5 collective-permute-start.3
  16.4 0.7 collective-permute-done.2
  17.1 0.2 collective-permute-done.3
  17.3 0.2 maximum_select_fusion
  17.5 0.1 slice_multiply_fusion
  17.6 0.2 fusion.4
  17.8 0.7 multiply_reduce_fusion.4
  18.5 40.5 %all-reduce.2 = (f32[]{:T(128)}, f32[]{:T(128)}) all-reduce(f32[]{:T(128)} %get-tuple-element.3, f32[]{:T(128)} %get-tuple-element.2), channel_id=1, replica_groups=mesh['lon'=16,'lat'=2] {'lon','lat'}, use_global_device_ids=true, to_apply=%region_1.2 | all-reduce | flops 2 | bytes 16 | tf_op jit(solution)/shard_map/psum | solution.py:87
  60.3 0.1 slice_divide_fusion.1
  60.4 2.3 %collective-permute-start.5 = (f32[1,512]{1,0:T(1,128)S(1)}, f32[1,512]{1,0:T(1,128)S(1)}, u32[]{:S(2)}, u32[]{:S(2)}) collective-permute-start(f32[1,512]{1,0:T(1,128)S(1)} %get-tuple-element.43), channel_id=1, source_target_pairs={{0,2},{2,4},{4,6},{6,8},{8,10},{10,12},{12,14},{14,16},{16,18},{18... | collective-permute-start | bytes 6152 | tf_op jit(solution)/shard_map/ppermute | solution.py:17
  62.8 3.3 %collective-permute-start.4 = (f32[1,512]{1,0:T(1,128)S(1)}, f32[1,512]{1,0:T(1,128)S(1)}, u32[]{:S(2)}, u32[]{:S(2)}) collective-permute-start(f32[1,512]{1,0:T(1,128)S(1)} %get-tuple-element.44), channel_id=1, source_target_pairs={{2,0},{4,2},{6,4},{8,6},{10,8},{12,10},{14,12},{16,14},{18,16},{20... | collective-permute-start | bytes 6152 | tf_op jit(solution)/shard_map/ppermute | solution.py:20
  66.1 1.6 collective-permute-done.5
  67.7 0.0 collective-permute-done.4
  67.7 0.1 pad_maximum_fusion.24
  67.8 0.0 collective-permute-start.6
  67.8 0.5 collective-permute-start.7
  68.3 0.7 collective-permute-done.6
  68.9 0.2 collective-permute-done.7
  69.1 0.8 multiply_reduce_fusion.2
  69.9 40.3 %all-reduce.1 = (f32[]{:T(128)}, f32[]{:T(128)}) all-reduce(f32[]{:T(128)} %get-tuple-element.7, f32[]{:T(128)} %get-tuple-element.6), channel_id=1, replica_groups=mesh['lon'=16,'lat'=2] {'lon','lat'}, use_global_device_ids=true, to_apply=%region_5.6 | all-reduce | flops 2 | bytes 16 | tf_op jit(solution)/shard_map/psum | solution.py:87
  114.5 0.1 slice_divide_fusion
  114.6 2.3 %collective-permute-start.9 = (f32[1,512]{1,0:T(1,128)S(1)}, f32[1,512]{1,0:T(1,128)S(1)}, u32[]{:S(2)}, u32[]{:S(2)}) collective-permute-start(f32[1,512]{1,0:T(1,128)S(1)} %get-tuple-element.41), channel_id=1, source_target_pairs={{0,2},{2,4},{4,6},{6,8},{8,10},{10,12},{12,14},{14,16},{16,18},{18... | collective-permute-start | bytes 6152 | tf_op jit(solution)/shard_map/ppermute | solution.py:17
  117.0 3.3 %collective-permute-start.8 = (f32[1,512]{1,0:T(1,128)S(1)}, f32[1,512]{1,0:T(1,128)S(1)}, u32[]{:S(2)}, u32[]{:S(2)}) collective-permute-start(f32[1,512]{1,0:T(1,128)S(1)} %get-tuple-element.42), channel_id=1, source_target_pairs={{2,0},{4,2},{6,4},{8,6},{10,8},{12,10},{14,12},{16,14},{18,16},{20... | collective-permute-start | bytes 6152 | tf_op jit(solution)/shard_map/ppermute | solution.py:20
  120.3 1.6 collective-permute-done.9
  121.9 0.0 collective-permute-done.8
  121.9 0.1 pad_maximum_fusion.21
  121.9 0.0 collective-permute-start.10
  122.0 0.5 collective-permute-start.11
  122.5 0.7 collective-permute-done.10
  123.1 0.2 collective-permute-done.11
  123.3 0.7 multiply_reduce_fusion
  124.0 40.4 %all-reduce = (f32[]{:T(128)}, f32[]{:T(128)}) all-reduce(f32[]{:T(128)} %get-tuple-element.5, f32[]{:T(128)} %get-tuple-element.4), channel_id=1, replica_groups=mesh['lon'=16,'lat'=2] {'lon','lat'}, use_global_device_ids=true, to_apply=%region_9.10 | all-reduce | flops 2 | bytes 16 | tf_op jit(solution)/shard_map/psum | solution.py:87
  168.2 0.7 multiply_subtract_fusion
  (19 shorter events, 0.1 us)
Async XLA Ops:
  0.6 1.1 copy-start
  0.6 2.5 %copy-start.6 = (f32[40]{0:T(128)S(1)}, f32[40]{0:T(128)}, u32[]{:S(2)}) copy-start(f32[40]{0:T(128)} %param.9) | copy-start | bytes 484
  0.7 2.5 %copy-start.1 = (f32[40,8,512]{2,1,0:T(8,128)S(1)}, f32[40,8,512]{2,1,0:T(8,128)}, u32[]{:S(2)}) copy-start(f32[40,8,512]{2,1,0:T(8,128)} %param.8) | copy-start | bytes 1966084
  4.0 0.7 copy-start.2
  4.7 0.7 copy-start.3
  5.4 0.7 copy-start.4
  6.1 0.7 copy-start.5
  6.9 8.8 %collective-permute-start = (f32[6,2,512]{2,1,0:T(2,128)S(1)}, f32[6,2,512]{2,1,0:T(2,128)S(1)}, u32[]{:S(2)}, u32[]{:S(2)}) collective-permute-start(f32[6,2,512]{2,1,0:T(2,128)S(1)} %get-tuple-element.33), channel_id=1, source_target_pairs={{0,2},{2,4},{4,6},{6,8},{8,10},{10,12},{12,14},{14,16},{16,18},{18... | collective-permute-start | bytes 73736 | tf_op jit(solution)/shard_map/ppermute | solution.py:17
  9.9 5.8 %collective-permute-start.1 = (f32[6,2,512]{2,1,0:T(2,128)S(1)}, f32[6,2,512]{2,1,0:T(2,128)S(1)}, u32[]{:S(2)}, u32[]{:S(2)}) collective-permute-start(f32[6,2,512]{2,1,0:T(2,128)S(1)} %get-tuple-element.34), channel_id=1, source_target_pairs={{2,0},{4,2},{6,4},{8,6},{10,8},{12,10},{14,12},{16,14},{18,16},{20... | collective-permute-start | bytes 73736 | tf_op jit(solution)/shard_map/ppermute | solution.py:20
  15.8 1.3 collective-permute-start.2
  15.9 1.4 collective-permute-start.3
  60.4 7.2 %collective-permute-start.5 = (f32[1,512]{1,0:T(1,128)S(1)}, f32[1,512]{1,0:T(1,128)S(1)}, u32[]{:S(2)}, u32[]{:S(2)}) collective-permute-start(f32[1,512]{1,0:T(1,128)S(1)} %get-tuple-element.43), channel_id=1, source_target_pairs={{0,2},{2,4},{4,6},{6,8},{8,10},{10,12},{12,14},{14,16},{16,18},{18... | collective-permute-start | bytes 6152 | tf_op jit(solution)/shard_map/ppermute | solution.py:17
  62.8 4.9 %collective-permute-start.4 = (f32[1,512]{1,0:T(1,128)S(1)}, f32[1,512]{1,0:T(1,128)S(1)}, u32[]{:S(2)}, u32[]{:S(2)}) collective-permute-start(f32[1,512]{1,0:T(1,128)S(1)} %get-tuple-element.44), channel_id=1, source_target_pairs={{2,0},{4,2},{6,4},{8,6},{10,8},{12,10},{14,12},{16,14},{18,16},{20... | collective-permute-start | bytes 6152 | tf_op jit(solution)/shard_map/ppermute | solution.py:20
  67.8 1.2 collective-permute-start.6
  67.8 1.3 collective-permute-start.7
  114.6 7.2 %collective-permute-start.9 = (f32[1,512]{1,0:T(1,128)S(1)}, f32[1,512]{1,0:T(1,128)S(1)}, u32[]{:S(2)}, u32[]{:S(2)}) collective-permute-start(f32[1,512]{1,0:T(1,128)S(1)} %get-tuple-element.41), channel_id=1, source_target_pairs={{0,2},{2,4},{4,6},{6,8},{8,10},{10,12},{12,14},{14,16},{16,18},{18... | collective-permute-start | bytes 6152 | tf_op jit(solution)/shard_map/ppermute | solution.py:17
  117.0 4.9 %collective-permute-start.8 = (f32[1,512]{1,0:T(1,128)S(1)}, f32[1,512]{1,0:T(1,128)S(1)}, u32[]{:S(2)}, u32[]{:S(2)}) collective-permute-start(f32[1,512]{1,0:T(1,128)S(1)} %get-tuple-element.42), channel_id=1, source_target_pairs={{2,0},{4,2},{6,4},{8,6},{10,8},{12,10},{14,12},{16,14},{18,16},{20... | collective-permute-start | bytes 6152 | tf_op jit(solution)/shard_map/ppermute | solution.py:20
  121.9 1.2 collective-permute-start.10
  122.0 1.3 collective-permute-start.11
where the time goes:
time: 170 us; the launch traced here: 169 us
  blocking collectives  121 us (71%)
  starting transfers between devices  20 us (12%)
  between operations  10.3 us (6%)
  waiting for transfers between devices  7.39 us (4%)
  local copies, waits for them, and re-layouts  3.97 us (2%)
  other arithmetic  3.8 us (2%)
  matrix products  2.22 us (1%)
    psum x3, blocking collectives, sums(): lax.psum((jnp.sum(residual * precond), jnp.sum(image * precond)), ('lon',...  121 us
    ppermute x6, starting transfers between devices, extended_2(): lax.ppermute(lax.slice_in_dim(block, 0, width, axis=dim), axis, backward)  11.3 us
    ppermute x6, starting transfers between devices, extended_2(): lax.ppermute(lax.slice_in_dim(block, block.shape[dim] - width, None, axis...  8.74 us
    ppermute x6, waiting for transfers between devices, extended_2(): lax.ppermute(lax.slice_in_dim(block, block.shape[dim] - width, None, axis...  5.9 us
    unnamed x16, local copies, waits for them, and re-layouts  3.92 us
  transfers between devices with their start and end apart: 12, of which 9 were waited for; matrix products, arithmetic and copies ran while one was open for 0% of the time, Pallas kernels for 0%

commit v1 on v0

--- a/solution.py
+++ b/solution.py
@@ -84,7 +84,9 @@
     diag = diag_mid[1:-1, 1:-1]
 
     def sums(residual, precond, image):
-        return lax.psum((jnp.sum(residual * precond), jnp.sum(image * precond)), ("lon", "lat"))
+        return lax.psum(
+            lax.psum((jnp.sum(residual * precond), jnp.sum(image * precond)), "lat"), "lon"
+        )
 
     surface = jnp.zeros_like(rhs)
     residual = rhs

time: 170 us -> 186 us (1.094)
  blocking collectives: 121 us -> 138 us
    psum x3 -> x6, blocking collectives: 121 us -> 138 us  [the longest x3 128 us: sums(): lax.psum(lax.psum((jnp.sum(residual * precond), jnp.sum(image * precond))...]
    ppermute x6, starting transfers between devices: 8.74 us -> 4.2 us  [extended_2(): lax.ppermute(lax.slice_in_dim(block, block.shape[dim] - width, None, axis...]
    ppermute x6, starting transfers between devices: 11.3 us -> 15.8 us  [extended_2(): lax.ppermute(lax.slice_in_dim(block, 0, width, axis=dim), axis, backward)]
where the time goes in v1:
time: 186 us
  blocking collectives  138 us (74%)
  starting transfers between devices  20 us (11%)
  between operations  10.4 us (6%)
  waiting for transfers between devices  7.39 us (4%)
  local copies, waits for them, and re-layouts  3.97 us (2%)
  other arithmetic  3.81 us (2%)
  matrix products  2.22 us (1%)
    psum x3, blocking collectives, sums(): lax.psum(lax.psum((jnp.sum(residual * precond), jnp.sum(image * precond))...  128 us
    ppermute x6, starting transfers between devices, extended_2(): lax.ppermute(lax.slice_in_dim(block, 0, width, axis=dim), axis, backward)  15.8 us
    psum x3, blocking collectives, sums(): lax.psum((jnp.sum(residual * precond), jnp.sum(image * precond)), 'lat')  9.36 us
    ppermute x6, waiting for transfers between devices, extended_2(): lax.ppermute(lax.slice_in_dim(block, block.shape[dim] - width, None, axis...  5.9 us
    ppermute x6, starting transfers between devices, extended_2(): lax.ppermute(lax.slice_in_dim(block, block.shape[dim] - width, None, axis...  4.2 us
    unnamed x16, local copies, waits for them, and re-layouts  3.92 us
  transfers between devices with their start and end apart: 12, of which 9 were waited for; matrix products, arithmetic and copies ran while one was open for 0% of the time, Pallas kernels for 0%

profile of v1, /device:TPU:0, one launch (start us, length us, event | category | flops | bytes accessed | tf_op | source)
XLA Modules:
  0.0 185.6 jit_solution(4934157503899498451)
XLA Ops:
  0.6 0.0 copy-start
  0.7 1.1 copy-done
  1.7 1.4 fusion.2
  3.2 0.8 fusion
  4.0 0.0 copy-start.2
  4.0 0.7 copy-done.2
  4.7 0.7 copy-done.3
  5.4 0.7 copy-done.4
  6.1 0.7 copy-done.5
  6.9 3.0 %collective-permute-start = (f32[6,2,512]{2,1,0:T(2,128)S(1)}, f32[6,2,512]{2,1,0:T(2,128)S(1)}, u32[]{:S(2)}, u32[]{:S(2)}) collective-permute-start(f32[6,2,512]{2,1,0:T(2,128)S(1)} %get-tuple-element.39), channel_id=1, source_target_pairs={{0,2},{2,4},{4,6},{6,8},{8,10},{10,12},{12,14},{14,16},{16,18},{18... | collective-permute-start | bytes 73736 | tf_op jit(solution)/shard_map/ppermute | solution.py:17
  9.9 4.1 %collective-permute-start.1 = (f32[6,2,512]{2,1,0:T(2,128)S(1)}, f32[6,2,512]{2,1,0:T(2,128)S(1)}, u32[]{:S(2)}, u32[]{:S(2)}) collective-permute-start(f32[6,2,512]{2,1,0:T(2,128)S(1)} %get-tuple-element.40), channel_id=1, source_target_pairs={{2,0},{4,2},{6,4},{8,6},{10,8},{12,10},{14,12},{16,14},{18,16},{20... | collective-permute-start | bytes 73736 | tf_op jit(solution)/shard_map/ppermute | solution.py:20
  14.0 1.7 collective-permute-done
  15.7 0.1 pad_maximum_fusion.2
  15.8 0.1 collective-permute-start.2
  15.9 0.5 collective-permute-start.3
  16.4 0.7 collective-permute-done.2
  17.1 0.2 collective-permute-done.3
  17.3 0.2 maximum_select_fusion
  17.5 0.1 slice_multiply_fusion
  17.6 0.2 fusion.4
  17.8 0.7 multiply_reduce_fusion.4
  18.5 3.1 %all-reduce.5 = (f32[]{:T(128)}, f32[]{:T(128)}) all-reduce(f32[]{:T(128)} %get-tuple-element.3, f32[]{:T(128)} %get-tuple-element.2), channel_id=1, replica_groups=mesh['lon'=16,'lat'=2] {'lat'}, use_global_device_ids=true, to_apply=%region_1.2 | all-reduce | flops 2 | bytes 16 | tf_op jit(solution)/shard_map/psum | solution.py:88
  21.6 42.8 %all-reduce.2 = (f32[]{:T(128)}, f32[]{:T(128)}) all-reduce(f32[]{:T(128)} %get-tuple-element.18, f32[]{:T(128)} %get-tuple-element.19), channel_id=1, replica_groups=mesh['lon'=16,'lat'=2] {'lon'}, use_global_device_ids=true, to_apply=%region_2.3 | all-reduce | flops 2 | bytes 16 | tf_op jit(solution)/shard_map/psum | solution.py:87
  65.8 0.1 slice_divide_fusion.1
  65.9 0.1 collective-permute-start.5
  66.0 5.6 %collective-permute-start.4 = (f32[1,512]{1,0:T(1,128)S(1)}, f32[1,512]{1,0:T(1,128)S(1)}, u32[]{:S(2)}, u32[]{:S(2)}) collective-permute-start(f32[1,512]{1,0:T(1,128)S(1)} %get-tuple-element.50), channel_id=1, source_target_pairs={{2,0},{4,2},{6,4},{8,6},{10,8},{12,10},{14,12},{16,14},{18,16},{20... | collective-permute-start | bytes 6152 | tf_op jit(solution)/shard_map/ppermute | solution.py:20
  71.6 1.6 collective-permute-done.5
  73.1 0.1 pad_maximum_fusion.24
  73.2 0.0 collective-permute-start.6
  73.2 0.5 collective-permute-start.7
  73.7 0.7 collective-permute-done.6
  74.4 0.2 collective-permute-done.7
  74.6 0.8 multiply_reduce_fusion.2
  75.3 3.2 %all-reduce.4 = (f32[]{:T(128)}, f32[]{:T(128)}) all-reduce(f32[]{:T(128)} %get-tuple-element.7, f32[]{:T(128)} %get-tuple-element.6), channel_id=1, replica_groups=mesh['lon'=16,'lat'=2] {'lat'}, use_global_device_ids=true, to_apply=%region_7.8 | all-reduce | flops 2 | bytes 16 | tf_op jit(solution)/shard_map/psum | solution.py:88
  78.5 42.9 %all-reduce.1 = (f32[]{:T(128)}, f32[]{:T(128)}) all-reduce(f32[]{:T(128)} %get-tuple-element.16, f32[]{:T(128)} %get-tuple-element.17), channel_id=1, replica_groups=mesh['lon'=16,'lat'=2] {'lon'}, use_global_device_ids=true, to_apply=%region_8.9 | all-reduce | flops 2 | bytes 16 | tf_op jit(solution)/shard_map/psum | solution.py:87
  125.8 0.1 slice_divide_fusion
  125.8 0.1 collective-permute-start.9
  125.9 5.6 %collective-permute-start.8 = (f32[1,512]{1,0:T(1,128)S(1)}, f32[1,512]{1,0:T(1,128)S(1)}, u32[]{:S(2)}, u32[]{:S(2)}) collective-permute-start(f32[1,512]{1,0:T(1,128)S(1)} %get-tuple-element.48), channel_id=1, source_target_pairs={{2,0},{4,2},{6,4},{8,6},{10,8},{12,10},{14,12},{16,14},{18,16},{20... | collective-permute-start | bytes 6152 | tf_op jit(solution)/shard_map/ppermute | solution.py:20
  131.5 1.6 collective-permute-done.9
  133.1 0.1 pad_maximum_fusion.21
  133.2 0.0 collective-permute-start.10
  133.2 0.5 collective-permute-start.11
  133.7 0.7 collective-permute-done.10
  134.3 0.2 collective-permute-done.11
  134.5 0.7 multiply_reduce_fusion
  135.2 3.1 %all-reduce.3 = (f32[]{:T(128)}, f32[]{:T(128)}) all-reduce(f32[]{:T(128)} %get-tuple-element.5, f32[]{:T(128)} %get-tuple-element.4), channel_id=1, replica_groups=mesh['lon'=16,'lat'=2] {'lat'}, use_global_device_ids=true, to_apply=%region_13.14 | all-reduce | flops 2 | bytes 16 | tf_op jit(solution)/shard_map/psum | solution.py:88
  138.3 42.8 %all-reduce = (f32[]{:T(128)}, f32[]{:T(128)}) all-reduce(f32[]{:T(128)} %get-tuple-element.14, f32[]{:T(128)} %get-tuple-element.15), channel_id=1, replica_groups=mesh['lon'=16,'lat'=2] {'lon'}, use_global_device_ids=true, to_apply=%region_14.15 | all-reduce | flops 2 | bytes 16 | tf_op jit(solution)/shard_map/psum | solution.py:87
  184.9 0.7 multiply_subtract_fusion
  (22 shorter events, 0.1 us)
Async XLA Ops:
  0.6 1.1 copy-start
  0.6 2.5 %copy-start.6 = (f32[40]{0:T(128)S(1)}, f32[40]{0:T(128)}, u32[]{:S(2)}) copy-start(f32[40]{0:T(128)} %param.9) | copy-start | bytes 484
  0.7 2.5 %copy-start.1 = (f32[40,8,512]{2,1,0:T(8,128)S(1)}, f32[40,8,512]{2,1,0:T(8,128)}, u32[]{:S(2)}) copy-start(f32[40,8,512]{2,1,0:T(8,128)} %param.8) | copy-start | bytes 1966084
  4.0 0.7 copy-start.2
  4.7 0.7 copy-start.3
  5.4 0.7 copy-start.4
  6.1 0.7 copy-start.5
  6.9 8.8 %collective-permute-start = (f32[6,2,512]{2,1,0:T(2,128)S(1)}, f32[6,2,512]{2,1,0:T(2,128)S(1)}, u32[]{:S(2)}, u32[]{:S(2)}) collective-permute-start(f32[6,2,512]{2,1,0:T(2,128)S(1)} %get-tuple-element.39), channel_id=1, source_target_pairs={{0,2},{2,4},{4,6},{6,8},{8,10},{10,12},{12,14},{14,16},{16,18},{18... | collective-permute-start | bytes 73736 | tf_op jit(solution)/shard_map/ppermute | solution.py:17
  9.9 5.8 %collective-permute-start.1 = (f32[6,2,512]{2,1,0:T(2,128)S(1)}, f32[6,2,512]{2,1,0:T(2,128)S(1)}, u32[]{:S(2)}, u32[]{:S(2)}) collective-permute-start(f32[6,2,512]{2,1,0:T(2,128)S(1)} %get-tuple-element.40), channel_id=1, source_target_pairs={{2,0},{4,2},{6,4},{8,6},{10,8},{12,10},{14,12},{16,14},{18,16},{20... | collective-permute-start | bytes 73736 | tf_op jit(solution)/shard_map/ppermute | solution.py:20
  15.8 1.3 collective-permute-start.2
  15.9 1.4 collective-permute-start.3
  65.9 7.2 %collective-permute-start.5 = (f32[1,512]{1,0:T(1,128)S(1)}, f32[1,512]{1,0:T(1,128)S(1)}, u32[]{:S(2)}, u32[]{:S(2)}) collective-permute-start(f32[1,512]{1,0:T(1,128)S(1)} %get-tuple-element.49), channel_id=1, source_target_pairs={{0,2},{2,4},{4,6},{6,8},{8,10},{10,12},{12,14},{14,16},{16,18},{18... | collective-permute-start | bytes 6152 | tf_op jit(solution)/shard_map/ppermute | solution.py:17
  66.0 7.2 %collective-permute-start.4 = (f32[1,512]{1,0:T(1,128)S(1)}, f32[1,512]{1,0:T(1,128)S(1)}, u32[]{:S(2)}, u32[]{:S(2)}) collective-permute-start(f32[1,512]{1,0:T(1,128)S(1)} %get-tuple-element.50), channel_id=1, source_target_pairs={{2,0},{4,2},{6,4},{8,6},{10,8},{12,10},{14,12},{16,14},{18,16},{20... | collective-permute-start | bytes 6152 | tf_op jit(solution)/shard_map/ppermute | solution.py:20
  73.2 1.2 collective-permute-start.6
  73.2 1.3 collective-permute-start.7
  125.8 7.2 %collective-permute-start.9 = (f32[1,512]{1,0:T(1,128)S(1)}, f32[1,512]{1,0:T(1,128)S(1)}, u32[]{:S(2)}, u32[]{:S(2)}) collective-permute-start(f32[1,512]{1,0:T(1,128)S(1)} %get-tuple-element.47), channel_id=1, source_target_pairs={{0,2},{2,4},{4,6},{6,8},{8,10},{10,12},{12,14},{14,16},{16,18},{18... | collective-permute-start | bytes 6152 | tf_op jit(solution)/shard_map/ppermute | solution.py:17
  125.9 7.2 %collective-permute-start.8 = (f32[1,512]{1,0:T(1,128)S(1)}, f32[1,512]{1,0:T(1,128)S(1)}, u32[]{:S(2)}, u32[]{:S(2)}) collective-permute-start(f32[1,512]{1,0:T(1,128)S(1)} %get-tuple-element.48), channel_id=1, source_target_pairs={{2,0},{4,2},{6,4},{8,6},{10,8},{12,10},{14,12},{16,14},{18,16},{20... | collective-permute-start | bytes 6152 | tf_op jit(solution)/shard_map/ppermute | solution.py:20
  133.2 1.2 collective-permute-start.10
  133.2 1.3 collective-permute-start.11
